TPU v7x, 32 devices: a whole 2x2x4 slice. The times are simulated.
32 devices in a mesh: gx: 4 (over z), gy: 2 (over y), gz: 4 (over x, core).
Axes of the slice: x: 2, y: 2, z: 4, core: 2. Of those that a mesh axis runs over, the one named last changes fastest.
Arguments:
- acts: bfloat16 [18816, 2048], P(('gx', 'gy', 'gz')), may hold values from -6 to 6
- saved_hidden: bfloat16 [18816, 512], P(('gx', 'gy', 'gz')), as said below
- grad_out: bfloat16 [18816, 2048], P(('gx', 'gy', 'gz')), may hold values from -6 to 6
- master_reduce: float32 [2048, 512], P(('gx', 'gy', 'gz')), may hold values from -60 to 60
- master_expand: float32 [2048, 512], P(('gx', 'gy', 'gz')), may hold values from -60 to 60
- velocity_reduce: float32 [2048, 512], P(('gx', 'gy', 'gz')), may hold values from -6 to 6
- velocity_expand: float32 [2048, 512], P(('gx', 'gy', 'gz')), may hold values from -6 to 6
Outputs:
- grad_in: bfloat16 [18816, 2048], P(('gx', 'gy', 'gz'))
- new_master_reduce: float32 [2048, 512], P(('gx', 'gy', 'gz'))
- new_master_expand: float32 [2048, 512], P(('gx', 'gy', 'gz'))
- new_velocity_reduce: float32 [2048, 512], P(('gx', 'gy', 'gz'))
- new_velocity_expand: float32 [2048, 512], P(('gx', 'gy', 'gz'))
- work_reduce: bfloat16 [2048, 512], replicated
- work_expand: bfloat16 [2048, 512], replicated
Inputs may be any that keep to these rules, and one draw needn't show every extreme that they name: `saved_hidden`: values are zero or positive, zero at about half of the entries.
All inputs are finite; a program needn't handle non-finite values.
Results may differ from a plain program's by a relative error of at most 0.0064.
Values may be sent and summed in bfloat16 or wider, within the bound.
A program may use at most 64 MiB of HBM per device.

v0:
```python
import jax
import jax.numpy as jnp
from jax import lax
from jax.sharding import PartitionSpec as P


def layer_update(master, grads, velocity, wsquare, gsquare):
    wnorm = jnp.sqrt(wsquare)
    gnorm = jnp.sqrt(gsquare)
    trust = wnorm / (gnorm + 5e-05 * wnorm)
    new_velocity = 0.9 * velocity + trust * (grads + 5e-05 * master)
    new_master = master - 0.1 * new_velocity
    return (new_master, new_velocity)


def shards(
    acts, saved_hidden, grad_out, master_reduce, master_expand, velocity_reduce, velocity_expand
):
    channels = grad_out.shape[1]
    middle = saved_hidden.shape[1]
    inv_c = 1.0 / float(channels) ** 0.5
    inv_m = 1.0 / float(middle) ** 0.5
    cur_reduce = master_reduce.astype(jnp.bfloat16)
    cur_expand = master_expand.astype(jnp.bfloat16)
    columns = grad_out
    summed = jnp.dot(
        columns,
        lax.all_gather(cur_expand, ("gx", "gy", "gz"), axis=0, tiled=True),
        preferred_element_type=jnp.float32,
    )
    grad_hidden = jnp.where(saved_hidden > 0, summed * inv_m, 0.0).astype(jnp.bfloat16)
    columns = grad_out
    g_expand = lax.psum_scatter(
        lax.dot_general(
            columns, saved_hidden, (((0,), (0,)), ((), ())), preferred_element_type=jnp.float32
        )
        * inv_m,
        ("gx", "gy", "gz"),
        scatter_dimension=0,
        tiled=True,
    )
    expand_parts = (jnp.sum(master_expand * master_expand), jnp.sum(g_expand * g_expand))
    expand_stats = lax.psum((expand_parts[0], expand_parts[1]), ("gx", "gy", "gz"))
    columns = acts
    g_reduce = lax.psum_scatter(
        lax.dot_general(
            columns, grad_hidden, (((0,), (0,)), ((), ())), preferred_element_type=jnp.float32
        )
        * inv_c,
        ("gx", "gy", "gz"),
        scatter_dimension=0,
        tiled=True,
    )
    back = lax.dot_general(
        grad_hidden,
        lax.all_gather(cur_reduce, ("gx", "gy", "gz"), axis=0, tiled=True),
        (((1,), (1,)), ((), ())),
        preferred_element_type=jnp.float32,
    )
    grad_in = (grad_out.astype(jnp.float32) + back * inv_c).astype(jnp.bfloat16)
    reduce_parts = (jnp.sum(master_reduce * master_reduce), jnp.sum(g_reduce * g_reduce))
    reduce_stats = lax.psum((reduce_parts[0], reduce_parts[1]), ("gx", "gy", "gz"))
    new_mr, new_vr = layer_update(
        master_reduce, g_reduce, velocity_reduce, reduce_stats[0], reduce_stats[1]
    )
    new_me, new_ve = layer_update(
        master_expand, g_expand, velocity_expand, expand_stats[0], expand_stats[1]
    )
    work_reduce, work_expand = (
        lax.all_gather(new_mr.astype(jnp.bfloat16), ("gx", "gy", "gz"), axis=0, tiled=True),
        lax.all_gather(new_me.astype(jnp.bfloat16), ("gx", "gy", "gz"), axis=0, tiled=True),
    )
    return (grad_in, new_mr, new_me, new_vr, new_ve, work_reduce, work_expand)


def solution(mesh):
    return jax.shard_map(
        shards,
        mesh=mesh,
        in_specs=(
            P(("gx", "gy", "gz"), None),
            P(("gx", "gy", "gz"), None),
            P(("gx", "gy", "gz"), None),
            P(("gx", "gy", "gz"), None),
            P(("gx", "gy", "gz"), None),
            P(("gx", "gy", "gz"), None),
            P(("gx", "gy", "gz"), None),
        ),
        out_specs=(
            P(("gx", "gy", "gz"), None),
            P(("gx", "gy", "gz"), None),
            P(("gx", "gy", "gz"), None),
            P(("gx", "gy", "gz"), None),
            P(("gx", "gy", "gz"), None),
            P(),
            P(),
        ),
        check_vma=False,
    )
```

profile of v0, /device:TPU:0, one launch (start us, length us, event | category | flops | bytes accessed | tf_op | source)
XLA Modules:
  0.0 581.7 jit_solution(12557865899018356745)
XLA Ops:
  7.2 0.0 all-gather.5.cloned.1.call-start
  7.2 2.4 multiply_reduce_fusion.2
  9.6 0.0 reduce-scatter.9.cloned.1.call-start
  9.7 5.6 convolution_multiply_fusion
  15.2 0.0 reduce-scatter.9.cloned.1.call-update
  15.3 0.0 reduce-scatter.7.cloned.1.call-start
  15.3 55.1 %all-gather.5.cloned.1.call-done = bf16[2048,512]{1,0:T(8,128)(2,1)} async-done(((bf16[64,512]{1,0:T(8,128)(2,1)}), bf16[2048,512]{1,0:T(8,128)(2,1)}) %all-gather.5.cloned.1.call-update) | async-done | bytes 2097168 | tf_op jit(solution)/shard_map/all_gather | solution.py:28
  70.4 3.9 fusion.1
  74.3 3.8 multiply_bitcast_fusion
  78.0 5.4 copy.43
  83.4 0.0 reduce-scatter.7.cloned.1.call-update
  83.4 0.0 all-gather.9.cloned.1.call-start
  83.5 0.8 copy-done.3
  84.3 0.6 multiply_reduce_fusion.3
  84.9 129.3 %reduce-scatter.9.cloned.1.call-done = f32[64,512]{1,0:T(8,128)} async-done(((f32[2048,512]{1,0:T(8,128)}), f32[64,512]{1,0:T(8,128)}) %reduce-scatter.9.cloned.1.call-update) | async-done | bytes 131088 | tf_op jit(solution)/shard_map/reduce_scatter | solution.py:33
  214.3 1.0 copy.46
  215.3 0.7 multiply_reduce_fusion
  216.0 139.2 %reduce-scatter.7.cloned.1.call-done = f32[64,512]{1,0:T(8,128)} async-done(((f32[2048,512]{1,0:T(8,128)}), f32[64,512]{1,0:T(8,128)}) %reduce-scatter.7.cloned.1.call-update) | async-done | bytes 131088 | tf_op jit(solution)/shard_map/reduce_scatter | solution.py:45
  355.1 1.0 copy.44
  356.2 0.7 multiply_reduce_fusion.1
  356.8 37.2 %all-reduce = (f32[]{:T(128)}, f32[]{:T(128)}, f32[]{:T(128)}, f32[]{:T(128)}) all-reduce(f32[]{:T(128)} %multiply_reduce_fusion.3, f32[]{:T(128)} %multiply_reduce_fusion.1, f32[]{:T(128)} %get-tuple-element.32, f32[]{:T(128)} %multiply_reduce_fusion), channel_id=1, replica_groups=mesh['gx'=4,'gy'=2,'gz'=4] {'gx','gy','gz'}, use_global_device_ids=true, to_apply=%region_1.2 | all-reduce | flops 4 | bytes 32 | tf_op jit(solution)/shard_map/psum | solution.py:62
  395.5 1.8 fusion.3
  397.2 0.0 all-gather.7.cloned.1.call-start
  397.3 0.5 all-gather.7.cloned.1.call-update
  397.8 0.0 all-gather.11.cloned.1.call-start
  399.3 1.7 fusion.2
  401.1 53.1 %all-gather.9.cloned.1.call-done = bf16[2048,512]{1,0:T(8,128)(2,1)} async-done(((bf16[64,512]{1,0:T(8,128)(2,1)}), bf16[2048,512]{1,0:T(8,128)(2,1)}) %all-gather.9.cloned.1.call-update) | async-done | bytes 2097168 | tf_op jit(solution)/shard_map/all_gather | solution.py:70
  454.2 58.4 %all-gather.7.cloned.1.call-done = bf16[2048,512]{1,0:T(8,128)(2,1)} async-done(((bf16[64,512]{1,0:T(8,128)(2,1)}), bf16[2048,512]{1,0:T(8,128)(2,1)}) %all-gather.7.cloned.1.call-update) | async-done | bytes 2097168 | tf_op jit(solution)/shard_map/all_gather | solution.py:56
  512.5 5.2 add_convert_fusion
  517.7 52.6 %all-gather.11.cloned.1.call-done = bf16[2048,512]{1,0:T(8,128)(2,1)} async-done(((bf16[64,512]{1,0:T(8,128)(2,1)}), bf16[2048,512]{1,0:T(8,128)(2,1)}) %all-gather.11.cloned.1.call-update) | async-done | bytes 2097168 | tf_op jit(solution)/shard_map/all_gather | solution.py:71
  570.3 3.2 copy.49
  573.5 1.3 copy.50
  (10 shorter events, 0.1 us)
Async XLA Ops:
  7.2 67.1 %copy-start = (bf16[588,2048]{1,0:T(8,128)(2,1)S(1)}, bf16[588,2048]{1,0:T(8,128)(2,1)}, u32[]{:S(2)}) copy-start(bf16[588,2048]{1,0:T(8,128)(2,1)} %param.7) | copy-start | bytes 7225348
  7.2 63.2 %all-gather.5.cloned.1.call-start = ((), (), s32[]{:S(2)}) async-start(), calls=%async_computation.2 | async-start | bytes 2162688 | tf_op jit(solution)/shard_map/all_gather | solution.py:28
  9.6 204.7 %reduce-scatter.9.cloned.1.call-start = ((), (), s32[]{:S(2)}) async-start(), calls=%async_computation.7 | async-start | bytes 4325376 | tf_op jit(solution)/shard_map/reduce_scatter | solution.py:33
  15.3 339.9 %reduce-scatter.7.cloned.1.call-start = ((), (), s32[]{:S(2)}) async-start(), calls=%async_computation.6 | async-start | bytes 4325376 | tf_op jit(solution)/shard_map/reduce_scatter | solution.py:45
  83.4 0.9 copy-start.3
  83.4 315.9 %copy-start.2 = (f32[64,512]{1,0:T(8,128)S(1)}, f32[64,512]{1,0:T(8,128)}, u32[]{:S(2)}) copy-start(f32[64,512]{1,0:T(8,128)} %param.11) | copy-start | bytes 393220
  83.4 370.7 %all-gather.9.cloned.1.call-start = ((), (), s32[]{:S(2)}) async-start(), calls=%async_computation.4 | async-start | bytes 2162688 | tf_op jit(solution)/shard_map/all_gather | solution.py:70
  397.2 115.3 %all-gather.7.cloned.1.call-start = ((), (), s32[]{:S(2)}) async-start(), calls=%async_computation.3 | async-start | bytes 2162688 | tf_op jit(solution)/shard_map/all_gather | solution.py:56
  397.8 172.5 %all-gather.11.cloned.1.call-start = ((), (), s32[]{:S(2)}) async-start(), calls=%async_computation.5 | async-start | bytes 2162688 | tf_op jit(solution)/shard_map/all_gather | solution.py:71
  570.3 3.2 copy-start.1
Sparse Core Ops, SparseCore 0:
  11.4 58.9 all-gather.4
  72.6 141.5 reduce-scatter.8
  216.6 138.5 reduce-scatter.6
  397.4 56.7 all-gather.8
  457.5 55.0 all-gather.6
  515.3 55.0 all-gather.10
where the time goes:
time: 582 us
  waiting for transfers between devices  488 us (84%)
  blocking collectives  37.2 us (6%)
  matrix products  18.4 us (3%)
  between operations  17 us (3%)
  local copies, waits for them, and re-layouts  12.8 us (2%)
  other arithmetic  7.81 us (1%)
    reduce_scatter x1, waiting for transfers between devices, shards(): lax.psum_scatter(lax.dot_general(columns, grad_hidden, (((0,), (0,)), (()...  139 us
    reduce_scatter x1, waiting for transfers between devices, shards(): lax.psum_scatter(lax.dot_general(columns, saved_hidden, (((0,), (0,)), ((...  129 us
    all_gather x1, waiting for transfers between devices, shards(): lax.all_gather(cur_reduce, ('gx', 'gy', 'gz'), axis=0, tiled=True)  58.4 us
    all_gather x1, waiting for transfers between devices, shards(): lax.all_gather(cur_expand, ('gx', 'gy', 'gz'), axis=0, tiled=True)  55.1 us
    all_gather x1, waiting for transfers between devices, shards(): lax.all_gather(new_mr.astype(jnp.bfloat16), ('gx', 'gy', 'gz'), axis=0, t...  53.1 us
    all_gather x1, waiting for transfers between devices, shards(): lax.all_gather(new_me.astype(jnp.bfloat16), ('gx', 'gy', 'gz'), axis=0, t...  52.6 us
    psum x1, blocking collectives, shards(): lax.psum((reduce_parts[0], reduce_parts[1]), ('gx', 'gy', 'gz'))  37.2 us
    unnamed x13, local copies, waits for them, and re-layouts  12.8 us
  transfers between devices with their start and end apart: 6, of which 6 were waited for; matrix products, arithmetic and copies ran while one was open for 5% of the time, Pallas kernels for 0%

commit v1 on v0

v1 whole, which is shorter than its diff:
```python
import functools

import jax
import jax.numpy as jnp
from jax import lax
from jax.experimental import pallas as pl
from jax.experimental.pallas import tpu as pltpu
from jax.sharding import PartitionSpec as P

AXES = ("gx", "gy", "gz")
MESH = pl.DeviceIdType.MESH
SLABS = 2


class Plan:
    def __init__(self, shape):
        self.sizes = dict(shape)
        self.factors = []
        for axis in reversed(AXES):
            stride = 1
            while stride < self.sizes[axis]:
                self.factors.append((axis, stride))
                stride *= 2
            assert stride == self.sizes[axis]
        self.n = len(self.factors)

    def order(self, slab):
        order = list(range(self.n))
        if slab % 2 and self.n > 2:
            order[1], order[2] = order[2], order[1]
        return order

    def digits(self):
        me = {a: lax.axis_index(a) for a in AXES}
        digits = [lax.rem(me[a] // s, 2) for a, s in self.factors]
        peers = [{a: me[a] + (1 - 2 * d) * s} for (a, s), d in zip(self.factors, digits)]
        return digits, peers

    def axis_peers(self, axis):
        me, n = lax.axis_index(axis), self.sizes[axis]
        return [{axis: lax.rem(me + j, n)} for j in range(1, n)]


def enter(plan):
    barrier = pltpu.get_barrier_semaphore()
    count = 0
    for axis in AXES:
        for peer in plan.axis_peers(axis):
            pl.semaphore_signal(barrier, inc=1, device_id=peer, device_id_type=MESH)
            count += 1
    pl.semaphore_wait(barrier, count)


def remote(src, dst, send, recv, peer):
    return pltpu.make_async_remote_copy(
        src_ref=src, dst_ref=dst, send_sem=send, recv_sem=recv,
        device_id=peer, device_id_type=MESH,
    )


def gather_stage(plan, digits, peers, t, stream, work, send, recv):
    layer, slab = stream
    order = plan.order(slab)
    held = order[t + 1 :]
    region = tuple(
        slice(None) if k in held else digits[k] for k in reversed(range(plan.n))
    )
    cols = work[layer].shape[-1] // SLABS
    part = work[layer].at[region + (slice(None), pl.ds(slab * cols, cols))]
    at = layer * SLABS + slab
    return remote(part, part, send.at[t, at], recv.at[t, at], peers[order[t]])


def gather(plan, digits, peers, streams, work, send, recv):
    copies = {}
    for t in reversed(range(plan.n)):
        for stream in streams:
            if t < plan.n - 1:
                copies[t + 1, stream].wait_recv()
            copy = gather_stage(plan, digits, peers, t, stream, work, send, recv)
            copy.start()
            copies[t, stream] = copy
    for stream in streams:
        copies[0, stream].wait_recv()
    for copy in copies.values():
        copy.wait_send()


def own_block(plan, digits):
    return tuple(digits[k] for k in reversed(range(plan.n)))


def gather_kernel(plan, mr, me, work_r, work_e, send, recv):
    digits, peers = plan.digits()
    own = own_block(plan, digits)
    work_r[own] = mr[...].astype(jnp.bfloat16)
    work_e[own] = me[...].astype(jnp.bfloat16)
    enter(plan)
    streams = [(layer, slab) for layer in (1, 0) for slab in range(SLABS)]
    gather(plan, digits, peers, streams, (work_r, work_e), send, recv)


def update_kernel(
    plan, pr, pe, mr, me, vr, ve,
    new_mr, new_me, new_vr, new_ve, work_r, work_e,
    total, sends, recvs, sums, shares, grads,
    rs_send, rs_recv, ag_send, ag_recv, n_send, n_recv,
):
    digits, peers = plan.digits()
    enter(plan)
    partial = (pr, pe)
    cols = pr.shape[-1] // SLABS
    streams = [(layer, slab) for layer in (0, 1) for slab in range(SLABS)]
    copies = {}
    last = plan.n - 1

    def position(order, t):
        rem = [k for k in reversed(range(plan.n)) if k not in order[:t]]
        at = rem.index(order[t])
        return 2 ** (len(rem) - at - 1)

    def kept(stream, t, bit, i):
        layer, slab = stream
        post = position(plan.order(slab), t)
        at = (i // post * 2 + bit) * post + i % post
        if t == 0:
            return partial[layer][at, :, pl.ds(slab * cols, cols)]
        return total[t - 1][layer * SLABS + slab, at]

    for t in range(plan.n):
        blocks = 2 ** (plan.n - t - 1)
        for stream in streams:
            layer, slab = stream
            s = layer * SLABS + slab
            order = plan.order(slab)
            if t > 0:
                copies[t - 1, s].wait_recv()
                before = digits[order[t - 1]]

                def add(i, c, stream=stream, s=s, t=t, before=before):
                    total[t - 1][s, i] = kept(stream, t - 1, before, i) + recvs[t - 1][
                        s, i
                    ].astype(jnp.float32)
                    return c

                lax.fori_loop(0, 2 * blocks, add, 0)
            away = 1 - digits[order[t]]

            def pack(i, c, stream=stream, s=s, t=t, away=away):
                sends[t][s, i] = kept(stream, t, away, i).astype(jnp.bfloat16)
                return c

            lax.fori_loop(0, blocks, pack, 0)
            copy = remote(
                sends[t].at[s], recvs[t].at[s], rs_send.at[t, s], rs_recv.at[t, s],
                peers[order[t]],
            )
            copy.start()
            copies[t, s] = copy

    for stream in streams:
        layer, slab = stream
        s = layer * SLABS + slab
        copies[last, s].wait_recv()
        grads[layer, :, pl.ds(slab * cols, cols)] = kept(
            stream, last, digits[plan.order(slab)[last]], 0
        ) + recvs[last][s, 0].astype(jnp.float32)

    def square(x):
        x = x * x
        lanes = jnp.sum(x, axis=0, keepdims=True)
        width = lanes.shape[1]
        return sum(lanes[:, c : c + 128] for c in range(0, width, 128))

    rows = [square(mr[...]), square(grads[0]), square(me[...]), square(grads[1])]
    sums[0] = jnp.concatenate(rows + [jnp.zeros((4, 128), jnp.float32)], axis=0)
    small, slot = [], 0
    for a, axis in enumerate(AXES):
        mine = []
        for peer in plan.axis_peers(axis):
            copy = remote(sums.at[a], shares.at[slot], n_send.at[slot], n_recv.at[slot], peer)
            copy.start()
            mine.append((copy, slot))
            slot += 1
        whole = sums[a]
        for copy, at in mine:
            copy.wait_recv()
            whole = whole + shares[at]
        sums[a + 1] = whole
        small += [copy for copy, _ in mine]
    stats = jnp.sum(sums[len(AXES)], axis=1, keepdims=True)

    own = own_block(plan, digits)
    for layer, (m, v, out_m, out_v, work) in enumerate(
        ((mr, vr, new_mr, new_vr, work_r), (me, ve, new_me, new_ve, work_e))
    ):
        wnorm = jnp.sqrt(stats[2 * layer : 2 * layer + 1])
        gnorm = jnp.sqrt(stats[2 * layer + 1 : 2 * layer + 2])
        trust = wnorm / (gnorm + 5e-05 * wnorm)
        velocity = 0.9 * v[...] + trust * (grads[layer] + 5e-05 * m[...])
        master = m[...] - 0.1 * velocity
        out_v[...] = velocity
        out_m[...] = master
        work[own] = master.astype(jnp.bfloat16)

    gather(plan, digits, peers, streams, (work_r, work_e), ag_send, ag_recv)
    for copy in list(copies.values()) + small:
        copy.wait_send()


VMEM = pl.BlockSpec(memory_space=pltpu.VMEM)


def all_gathered(plan, mr, me):
    rows, width = mr.shape
    shape = jax.ShapeDtypeStruct((2,) * plan.n + (rows, width), jnp.bfloat16)
    sems = pltpu.SemaphoreType.DMA((plan.n, 2 * SLABS))
    out = pl.pallas_call(
        functools.partial(gather_kernel, plan),
        out_shape=(shape, shape),
        in_specs=[VMEM] * 2,
        out_specs=(VMEM, VMEM),
        scratch_shapes=[sems, sems],
        compiler_params=pltpu.CompilerParams(collective_id=0, has_side_effects=True),
        name="gather_weights",
    )(mr, me)
    return [x.reshape(-1, width) for x in out]


def updated(plan, pr, pe, mr, me, vr, ve):
    rows, width = mr.shape
    n, streams = plan.n, 2 * SLABS
    cols = width // SLABS
    f32, bf16 = jnp.float32, jnp.bfloat16
    work = jax.ShapeDtypeStruct((2,) * n + (rows, width), bf16)
    shard = jax.ShapeDtypeStruct((rows, width), f32)
    sems = pltpu.SemaphoreType.DMA((n, streams))
    slots = sum(plan.sizes[a] - 1 for a in AXES)
    half = [2 ** (n - t - 1) for t in range(n)]
    out = pl.pallas_call(
        functools.partial(update_kernel, plan),
        out_shape=(shard,) * 4 + (work,) * 2,
        in_specs=[VMEM] * 6,
        out_specs=(VMEM,) * 6,
        scratch_shapes=[
            [pltpu.VMEM((streams, b, rows, cols), f32) for b in half],
            [pltpu.VMEM((streams, b, rows, cols), bf16) for b in half],
            [pltpu.VMEM((streams, b, rows, cols), bf16) for b in half],
            pltpu.VMEM((len(AXES) + 1, 8, 128), f32),
            pltpu.VMEM((slots, 8, 128), f32),
            pltpu.VMEM((2, rows, width), f32),
            sems, sems, sems, sems,
            pltpu.SemaphoreType.DMA((slots,)),
            pltpu.SemaphoreType.DMA((slots,)),
        ],
        compiler_params=pltpu.CompilerParams(collective_id=1, has_side_effects=True),
        name="reduce_update_gather",
    )(pr.reshape(-1, rows, width), pe.reshape(-1, rows, width), mr, me, vr, ve)
    return out[:4] + tuple(x.reshape(-1, width) for x in out[4:])


def shards(
    plan, acts, saved_hidden, grad_out, master_reduce, master_expand,
    velocity_reduce, velocity_expand,
):
    inv_c = 1.0 / float(grad_out.shape[1]) ** 0.5
    inv_m = 1.0 / float(saved_hidden.shape[1]) ** 0.5
    f32 = jnp.float32
    cur_reduce, cur_expand = all_gathered(plan, master_reduce, master_expand)
    summed = jnp.dot(grad_out, cur_expand, preferred_element_type=f32)
    grad_hidden = jnp.where(saved_hidden > 0, summed * inv_m, 0.0).astype(jnp.bfloat16)
    over_rows = (((0,), (0,)), ((), ()))
    g_expand = lax.dot_general(grad_out, saved_hidden, over_rows, preferred_element_type=f32) * inv_m
    g_reduce = lax.dot_general(acts, grad_hidden, over_rows, preferred_element_type=f32) * inv_c
    back = lax.dot_general(
        grad_hidden, cur_reduce, (((1,), (1,)), ((), ())), preferred_element_type=f32
    )
    grad_in = (grad_out.astype(f32) + back * inv_c).astype(jnp.bfloat16)
    new_mr, new_me, new_vr, new_ve, work_reduce, work_expand = updated(
        plan, g_reduce, g_expand, master_reduce, master_expand, velocity_reduce, velocity_expand
    )
    return (grad_in, new_mr, new_me, new_vr, new_ve, work_reduce, work_expand)


def solution(mesh):
    rows = P(AXES, None)
    return jax.shard_map(
        functools.partial(shards, Plan(mesh.shape)),
        mesh=mesh,
        in_specs=(rows,) * 7,
        out_specs=(rows,) * 5 + (P(), P()),
        check_vma=False,
    )
```

time: 582 us -> 150 us (0.26)
  waiting for transfers between devices: 488 us -> 0 us
  Pallas kernels: 0 us -> 117 us
  blocking collectives: 37.2 us -> 0 us
  between operations: 17 us -> 0.72 us
  other arithmetic: 7.81 us -> 0 us
    reduce_scatter x2 -> x0, waiting for transfers between devices: 268 us -> none  [the longest x1 139 us: shards(): lax.psum_scatter(lax.dot_general(columns, grad_hidden, (((0,), (0,)), (()...]
    all_gather x4 -> x0, waiting for transfers between devices: 219 us -> none  [the longest x1 58.4 us: shards(): lax.all_gather(cur_reduce, ('gx', 'gy', 'gz'), axis=0, tiled=True)]
    pallas_call x0 -> x2, Pallas kernels: none -> 117 us  [the longest x1 78.6 us: updated(): pl.pallas_call(functools.partial(update_kernel, plan), out_shape=(shard,)...]
    psum x1 -> x0, blocking collectives: 37.2 us -> none  [shards(): lax.psum((reduce_parts[0], reduce_parts[1]), ('gx', 'gy', 'gz'))]
    unnamed x13 -> x16, local copies, waits for them, and re-layouts: 12.8 us -> 10.8 us
  transfers between devices with their start and end apart: 6 -> 0, of which waited for: 6 -> 0; matrix products, arithmetic and copies ran while one was open for 5% -> 0% of each run, Pallas kernels for 0% -> 0%
where the time goes in v1:
time: 150 us
  Pallas kernels  117 us (78%)
  matrix products  16.3 us (11%)
  local copies, waits for them, and re-layouts  16.2 us (11%)
    pallas_call x1, Pallas kernels, updated(): pl.pallas_call(functools.partial(update_kernel, plan), out_shape=(shard,)...  78.6 us
    pallas_call x1, Pallas kernels, all_gathered(): pl.pallas_call(functools.partial(gather_kernel, plan), out_shape=(shape,...  38.3 us
    unnamed x16, local copies, waits for them, and re-layouts  10.8 us
    dot_general x1, matrix products, shards(): lax.dot_general(grad_out, saved_hidden, over_rows, preferred_element_type...  5.74 us
    mul x1, local copies, waits for them, and re-layouts, shards(): lax.dot_general(acts, grad_hidden, over_rows, preferred_element_type=f32)  5.38 us
    dot_general x1, matrix products, shards(): summed = jnp.dot(grad_out, cur_expand, preferred_element_type=f32)  3.9 us
    dot_general x1, matrix products, shards(): lax.dot_general(acts, grad_hidden, over_rows, preferred_element_type=f32)  3.79 us

profile of v1, /device:TPU:0, one launch (start us, length us, event | category | flops | bytes accessed | tf_op | source)
XLA Modules:
  0.0 150.1 jit_solution(3432337796191162423)
XLA Ops:
  0.6 0.0 copy-start
  0.6 0.0 copy-start.4
  0.7 5.7 %convolution_multiply_fusion = f32[2048,512]{1,0:T(8,128)} fusion(bf16[588,2048]{1,0:T(8,128)(2,1)} %param.9, bf16[588,512]{1,0:T(8,128)(2,1)} %param.8), kind=kOutput, calls=%fused_computation.2 | convolution fusion | flops 1234173952 | bytes 7204864 | tf_op jit(solution)/shard_map/dot_general | solution.py:273
  6.4 38.3 %gather_weights.1 = (bf16[2,2,2,2,2,64,512]{6,5,4,3,2,1,0:T(8,128)(2,1)}, bf16[2,2,2,2,2,64,512]{6,5,4,3,2,1,0:T(8,128)(2,1)}) custom-call(f32[64,512]{1,0:T(8,128)} %mr.3, f32[64,512]{1,0:T(8,128)} %me.3), custom_call_target="tpu_custom_call" | custom-call | tf_op jit(solution)/shard_map/gather_weights/pallas_call | solution.py:218
  44.7 0.0 copy-done.4
  44.7 0.0 copy-start.2
  44.7 0.0 copy-start.3
  44.7 3.9 %fusion.2 = bf16[588,512]{1,0:T(8,128)(2,1)S(1)} fusion(bf16[2048,512]{1,0:T(8,128)(2,1)} %bitcast.27, bf16[588,2048]{1,0:T(8,128)(2,1)} %param.9, bf16[588,512]{1,0:T(8,128)(2,1)S(1)} %copy-done.4), kind=kOutput, calls=%fused_computation.6 | convolution fusion | flops 1234329600 | bytes 5709824 | tf_op jit(solution)/shard_map/dot_general | solution.py:270
  48.6 0.0 copy-done.2
  48.6 0.0 copy-done.3
  48.6 2.9 %add_convert_fusion = bf16[588,2048]{1,0:T(8,128)(2,1)} fusion(bf16[588,2048]{1,0:T(8,128)(2,1)S(1)} %copy-done.2, bf16[588,512]{1,0:T(8,128)(2,1)S(1)} %fusion.2, bf16[2048,512]{1,0:T(8,128)(2,1)S(1)} %bitcast.26), kind=kOutput, calls=%fused_computation | convolution fusion | flops 1237942272 | bytes 7516160 | tf_op jit(solution)/shard_map/dot_general | solution.py:275
  51.5 0.0 copy-done
  51.5 3.8 %multiply_bitcast_fusion = f32[2048,512]{0,1:T(8,128)} fusion(bf16[588,512]{1,0:T(8,128)(2,1)S(1)} %fusion.2, bf16[588,2048]{1,0:T(8,128)(2,1)S(1)} %copy-done), kind=kOutput, calls=%fused_computation.1 | convolution fusion | flops 1234173952 | bytes 7204864 | tf_op jit(solution)/shard_map/dot_general | solution.py:274
  55.3 5.4 %copy.14 = f32[2048,512]{1,0:T(8,128)} copy(f32[2048,512]{0,1:T(8,128)} %multiply_bitcast_fusion) | data formatting | bytes 8388608 | tf_op jit(solution)/shard_map/mul | solution.py:274
  60.7 78.6 %reduce_update_gather.1 = (f32[64,512]{1,0:T(8,128)}, f32[64,512]{1,0:T(8,128)}, f32[64,512]{1,0:T(8,128)}, f32[64,512]{1,0:T(8,128)}, bf16[2,2,2,2,2,64,512]{6,...) custom-call(f32[32,64,512]{2,1,0:T(8,128)} %bitcast.22, f32[32,64,512]{2,1,0:T(8,128)} %bitcast.23, ...), custom_call_target="tpu_custom_call" | custom-call | tf_op jit(solution)/shard_map/reduce_update_gather/pallas_call | solution.py:240
  139.3 1.6 %copy.21 = f32[64,512]{1,0:T(8,128)} copy(f32[64,512]{1,0:T(8,128)} %get-tuple-element.31) | data formatting | bytes 262144
  140.9 1.6 %copy.22 = f32[64,512]{1,0:T(8,128)} copy(f32[64,512]{1,0:T(8,128)} %get-tuple-element.32) | data formatting | bytes 262144
  142.5 0.0 copy-start.1
  142.5 1.7 %copy.23 = f32[64,512]{1,0:T(8,128)} copy(f32[64,512]{1,0:T(8,128)} %get-tuple-element.33) | data formatting | bytes 262144
  144.2 1.6 %copy.24 = f32[64,512]{1,0:T(8,128)} copy(f32[64,512]{1,0:T(8,128)} %get-tuple-element.34) | data formatting | bytes 262144
  145.7 3.0 %copy.25 = bf16[2048,512]{1,0:T(8,128)(2,1)} copy(bf16[2048,512]{1,0:T(8,128)(2,1)} %bitcast.25) | data formatting | bytes 4194304
  148.8 0.0 copy-done.1
  148.8 1.3 copy.26
Async XLA Ops:
  0.6 50.9 %copy-start = (bf16[588,2048]{1,0:T(8,128)(2,1)S(1)}, bf16[588,2048]{1,0:T(8,128)(2,1)}, u32[]{:S(2)}) copy-start(bf16[588,2048]{1,0:T(8,128)(2,1)} %param.7) | copy-start | bytes 7225348
  0.6 44.0 %copy-start.4 = (bf16[588,512]{1,0:T(8,128)(2,1)S(1)}, bf16[588,512]{1,0:T(8,128)(2,1)}, u32[]{:S(2)}) copy-start(bf16[588,512]{1,0:T(8,128)(2,1)} %param.8) | copy-start | bytes 1806340
  44.7 3.9 %copy-start.2 = (bf16[588,2048]{1,0:T(8,128)(2,1)S(1)}, bf16[588,2048]{1,0:T(8,128)(2,1)}, u32[]{:S(2)}) copy-start(bf16[588,2048]{1,0:T(8,128)(2,1)} %param.9) | copy-start | bytes 7225348
  44.7 3.9 %copy-start.3 = (bf16[2,2,2,2,2,64,512]{6,5,4,3,2,1,0:T(8,128)(2,1)S(1)}, bf16[2,2,2,2,2,64,512]{6,5,4,3,2,1,0:T(8,128)(2,1)}, u32[]{:S(2)}) copy-start(bf16[2,2,2,2,2,64,512]{6,5,4,3,2,1,0:T(8,128)(2,1)} %get-tuple-element.16) | copy-start | bytes 6291460
  142.5 6.3 %copy-start.1 = (bf16[2,2,2,2,2,64,512]{6,5,4,3,2,1,0:T(8,128)(2,1)S(1)}, bf16[2,2,2,2,2,64,512]{6,5,4,3,2,1,0:T(8,128)(2,1)}, u32[]{:S(2)}) copy-start(bf16[2,2,2,2,2,64,512]{6,5,4,3,2,1,0:T(8,128)(2,1)} %get-tuple-element.22) | copy-start | bytes 6291460

commit v2 on v0

v2 whole, which is shorter than its diff:
```python
import functools

import jax
import jax.numpy as jnp
from jax import lax
from jax.experimental import pallas as pl
from jax.experimental.pallas import tpu as pltpu
from jax.sharding import PartitionSpec as P

AXES = ("gx", "gy", "gz")
MESH = pl.DeviceIdType.MESH
SLABS = 2


class Plan:
    def __init__(self, shape):
        self.sizes = dict(shape)
        self.factors = []
        for axis in reversed(AXES):
            stride = 1
            while stride < self.sizes[axis]:
                self.factors.append((axis, stride))
                stride *= 2
            assert stride == self.sizes[axis]
        self.n = len(self.factors)

    def order(self, slab):
        order = list(range(self.n))
        if slab % 2 and self.n > 2:
            order[1], order[2] = order[2], order[1]
        return order

    def digits(self):
        me = {a: lax.axis_index(a) for a in AXES}
        digits = [lax.rem(me[a] // s, 2) for a, s in self.factors]
        peers = [{a: me[a] + (1 - 2 * d) * s} for (a, s), d in zip(self.factors, digits)]
        return digits, peers

    def axis_peers(self, axis):
        me, n = lax.axis_index(axis), self.sizes[axis]
        return [{axis: lax.rem(me + j, n)} for j in range(1, n)]


def enter(plan):
    barrier = pltpu.get_barrier_semaphore()
    count = 0
    for axis in AXES:
        for peer in plan.axis_peers(axis):
            pl.semaphore_signal(barrier, inc=1, device_id=peer, device_id_type=MESH)
            count += 1
    pl.semaphore_wait(barrier, count)


def remote(src, dst, send, recv, peer):
    return pltpu.make_async_remote_copy(
        src_ref=src, dst_ref=dst, send_sem=send, recv_sem=recv,
        device_id=peer, device_id_type=MESH,
    )


def own_block(plan, digits):
    return tuple(digits[k] for k in reversed(range(plan.n)))


def position(plan, order, t):
    rem = [k for k in reversed(range(plan.n)) if k not in order[:t]]
    return 2 ** (len(rem) - rem.index(order[t]) - 1)


class Gather:
    def __init__(self, plan, slab, where, work, send, recv, used):
        self.plan, self.slab, self.where, self.work = plan, slab, where, work
        self.send, self.recv, self.used = send, recv, used
        self.t, self.copy = plan.n - 1, None

    def step(self):
        assert self.t >= -1
        if self.copy is not None:
            self.copy.wait_recv()
        if self.t < 0:
            self.t = -2
            return
        digits, peers = self.where
        plan, t = self.plan, self.t
        order = plan.order(self.slab)
        held = order[t + 1 :]
        region = tuple(
            slice(None) if k in held else digits[k] for k in reversed(range(plan.n))
        )
        cols = self.work.shape[-1] // SLABS
        part = self.work.at[region + (slice(None), pl.ds(self.slab * cols, cols))]
        self.copy = remote(
            part, part, self.send.at[t, self.slab], self.recv.at[t, self.slab], peers[order[t]]
        )
        self.copy.start()
        self.used.append(self.copy)
        self.t = t - 1


class Scatter:
    def __init__(self, plan, slab, where, partial, total, sends, recvs, grad, send, recv, used):
        self.plan, self.slab, self.where, self.partial = plan, slab, where, partial
        self.total, self.sends, self.recvs, self.grad = total, sends, recvs, grad
        self.send, self.recv, self.used = send, recv, used
        self.t, self.copy = 0, None
        self.cols = partial.shape[-1] // SLABS

    def kept(self, t, bit, i):
        post = position(self.plan, self.plan.order(self.slab), t)
        at = (i // post * 2 + bit) * post + i % post
        if t == 0:
            return self.partial[at, :, pl.ds(self.slab * self.cols, self.cols)]
        return self.total[t - 1][self.slab, at]

    def step(self):
        digits, peers = self.where
        plan, t, s = self.plan, self.t, self.slab
        order = plan.order(s)
        sends, recvs, total = self.sends, self.recvs, self.total
        if t > 0:
            self.copy.wait_recv()
            before = digits[order[t - 1]]

            def summed(i):
                return self.kept(t - 1, before, i) + recvs[t - 1][s, i].astype(jnp.float32)

            if t == plan.n:
                self.grad[:, pl.ds(s * self.cols, self.cols)] = summed(0)
                return

            def add(i, c):
                total[t - 1][s, i] = summed(i)
                return c

            lax.fori_loop(0, 2 ** (plan.n - t), add, 0)
        away = 1 - digits[order[t]]

        def pack(i, c):
            sends[t][s, i] = self.kept(t, away, i).astype(jnp.bfloat16)
            return c

        lax.fori_loop(0, 2 ** (plan.n - t - 1), pack, 0)
        self.copy = remote(
            sends[t].at[s], recvs[t].at[s], self.send.at[t, s], self.recv.at[t, s],
            peers[order[t]],
        )
        self.copy.start()
        self.used.append(self.copy)
        self.t = t + 1


class Norms:
    def __init__(self, plan, sums, shares, send, recv, used):
        self.plan, self.sums, self.shares = plan, sums, shares
        self.send, self.recv, self.used = send, recv, used
        self.a, self.slot, self.mine = 0, 0, []

    def begin(self, m, g):
        def square(x):
            x = x * x
            lanes = jnp.sum(x, axis=0, keepdims=True)
            return sum(lanes[:, c : c + 128] for c in range(0, lanes.shape[1], 128))

        rows = [square(m), square(g), jnp.zeros((6, 128), jnp.float32)]
        self.sums[0] = jnp.concatenate(rows, axis=0)
        self.step()

    def step(self):
        if self.mine:
            whole = self.sums[self.a - 1]
            for copy, at in self.mine:
                copy.wait_recv()
                whole = whole + self.shares[at]
            self.sums[self.a] = whole
        self.mine = []
        if self.a == len(AXES):
            return
        for peer in self.plan.axis_peers(AXES[self.a]):
            copy = remote(
                self.sums.at[self.a], self.shares.at[self.slot],
                self.send.at[self.slot], self.recv.at[self.slot], peer,
            )
            copy.start()
            self.used.append(copy)
            self.mine.append((copy, self.slot))
            self.slot += 1
        self.a += 1

    def trust(self):
        stats = jnp.sum(self.sums[len(AXES)], axis=1, keepdims=True)
        wnorm, gnorm = jnp.sqrt(stats[0:1]), jnp.sqrt(stats[1:2])
        return wnorm / (gnorm + 5e-05 * wnorm)


def kernel(
    plan, acts, hidden, grad_out, mr, me, vr, ve,
    grad_hidden, cur_r, new_mr, new_me, new_vr, new_ve, work_r, work_e,
    cur_e, partial_r, partial_e, total_r, total_e, sends_r, sends_e, recvs_r, recvs_e,
    grad_r, grad_e, sums_r, sums_e, shares_r, shares_e,
    g_send, g_recv, s_send, s_recv, n_send, n_recv,
):
    where = digits, _ = plan.digits()
    own = own_block(plan, digits)
    used = []
    width = mr.shape[1]
    rows = mr.shape[0]
    channels = grad_out.shape[1]
    f32 = jnp.float32
    inv_c = 1.0 / float(channels) ** 0.5
    inv_m = 1.0 / float(width) ** 0.5

    def gathers(at, work):
        return [
            Gather(plan, s, where, work, g_send.at[at], g_recv.at[at], used)
            for s in range(SLABS)
        ]

    def scatters(at, partial, total, sends, recvs, grad):
        return [
            Scatter(
                plan, s, where, partial, total, sends, recvs, grad,
                s_send.at[at], s_recv.at[at], used,
            )
            for s in range(SLABS)
        ]

    gather_e, gather_r = gathers(0, cur_e), gathers(1, cur_r)
    final_e, final_r = gathers(2, work_e), gathers(3, work_r)
    scatter_e = scatters(0, partial_e, total_e, sends_e, recvs_e, grad_e)
    scatter_r = scatters(1, partial_r, total_r, sends_r, recvs_r, grad_r)
    norms_e = Norms(plan, sums_e, shares_e, n_send.at[0], n_recv.at[0], used)
    norms_r = Norms(plan, sums_r, shares_r, n_send.at[1], n_recv.at[1], used)

    def step(*groups):
        for group in groups:
            for task in group:
                task.step()

    pieces = 8
    wide = channels // pieces
    over_rows = (((0,), (0,)), ((), ()))

    def weight_grad(left, right, partial, scale, first, count):
        def piece(i, c):
            cols = left[:, pl.ds(pl.multiple_of(i * wide, wide), wide)]
            product = lax.dot_general(cols, right[...], over_rows, preferred_element_type=f32)
            blocks = wide // rows
            partial[pl.ds(i * blocks, blocks)] = (product * scale).reshape(blocks, rows, width)
            return c

        lax.fori_loop(first, first + count, piece, 0)

    def hidden_grad():
        cols = width // 2
        for c in range(0, width, cols):
            weights = cur_e[(slice(None),) * plan.n + (slice(None), pl.ds(c, cols))]
            summed = jnp.dot(
                grad_out[...], weights.reshape(channels, cols), preferred_element_type=f32
            )
            kept = hidden[:, c : c + cols].astype(f32) > 0
            grad_hidden[:, c : c + cols] = jnp.where(kept, summed * inv_m, 0.0).astype(
                jnp.bfloat16
            )

    def update(m, v, out_m, out_v, work, grad, norms):
        velocity = 0.9 * v[...] + norms.trust() * (grad[...] + 5e-05 * m[...])
        master = m[...] - 0.1 * velocity
        out_v[...] = velocity
        out_m[...] = master
        work[own] = master.astype(jnp.bfloat16)

    cur_r[own] = mr[...].astype(jnp.bfloat16)
    cur_e[own] = me[...].astype(jnp.bfloat16)
    enter(plan)

    step(gather_e)
    weight_grad(grad_out, hidden, partial_e, inv_m, 0, pieces // 4)
    step(gather_e, gather_r)
    weight_grad(grad_out, hidden, partial_e, inv_m, pieces // 4, pieces // 4)
    step(gather_e, gather_r)
    weight_grad(grad_out, hidden, partial_e, inv_m, pieces // 2, pieces // 2)
    step(scatter_e)
    for _ in range(plan.n - 3):
        step(gather_e)
    step(scatter_e)
    step(gather_e)
    hidden_grad()
    step(gather_r)
    weight_grad(acts, grad_hidden, partial_r, inv_c, 0, pieces)
    step(scatter_r)
    step(scatter_e)
    step(scatter_r)
    for _ in range(plan.n - 3):
        step(gather_r)
    for _ in range(plan.n - 2):
        step(scatter_e)
    norms_e.begin(me[...], grad_e[...])
    step(scatter_r)
    norms_e.step()
    step(gather_r)
    norms_e.step()
    step(scatter_r)
    norms_e.step()
    update(me, ve, new_me, new_ve, work_e, grad_e, norms_e)
    step(final_e)
    for _ in range(plan.n - 3):
        step(scatter_r)
    step(final_e)
    norms_r.begin(mr[...], grad_r[...])
    step(final_e)
    norms_r.step()
    norms_r.step()
    norms_r.step()
    update(mr, vr, new_mr, new_vr, work_r, grad_r, norms_r)
    step(final_r)
    step(final_e)
    for _ in range(plan.n - 3):
        step(final_r, final_e)
    step(final_r)
    step(final_r)
    step(final_r)
    for task in gather_e + gather_r + final_e + final_r:
        assert task.t == -2
    for copy in used:
        copy.wait_send()


VMEM = pl.BlockSpec(memory_space=pltpu.VMEM)


def fused(plan, acts, hidden, grad_out, mr, me, vr, ve):
    rows, width = mr.shape
    n = plan.n
    cols = width // SLABS
    f32, bf16 = jnp.float32, jnp.bfloat16
    work = jax.ShapeDtypeStruct((2,) * n + (rows, width), bf16)
    shard = jax.ShapeDtypeStruct((rows, width), f32)
    slots = sum(plan.sizes[a] - 1 for a in AXES)
    half = [2 ** (n - t - 1) for t in range(n)]

    def stages(dtype):
        return [pltpu.VMEM((SLABS, b, rows, cols), dtype) for b in half]

    sems = pltpu.SemaphoreType.DMA
    out = pl.pallas_call(
        functools.partial(kernel, plan),
        out_shape=(jax.ShapeDtypeStruct(hidden.shape, bf16), work) + (shard,) * 4 + (work,) * 2,
        in_specs=[VMEM] * 7,
        out_specs=(VMEM,) * 8,
        scratch_shapes=[
            pltpu.VMEM((2,) * n + (rows, width), bf16),
            pltpu.VMEM((2**n, rows, width), f32),
            pltpu.VMEM((2**n, rows, width), f32),
            stages(f32), stages(f32), stages(bf16), stages(bf16), stages(bf16), stages(bf16),
            pltpu.VMEM((rows, width), f32),
            pltpu.VMEM((rows, width), f32),
            pltpu.VMEM((len(AXES) + 1, 8, 128), f32),
            pltpu.VMEM((len(AXES) + 1, 8, 128), f32),
            pltpu.VMEM((slots, 8, 128), f32),
            pltpu.VMEM((slots, 8, 128), f32),
            sems((4, n, SLABS)), sems((4, n, SLABS)),
            sems((2, n, SLABS)), sems((2, n, SLABS)),
            sems((2, slots)), sems((2, slots)),
        ],
        compiler_params=pltpu.CompilerParams(collective_id=0, has_side_effects=True),
        name="fused_step",
    )(acts, hidden, grad_out, mr, me, vr, ve)
    return [x.reshape(-1, width) if x.ndim > 2 else x for x in out]


def shards(
    plan, acts, saved_hidden, grad_out, master_reduce, master_expand,
    velocity_reduce, velocity_expand,
):
    inv_c = 1.0 / float(grad_out.shape[1]) ** 0.5
    f32 = jnp.float32
    grad_hidden, cur_reduce, *rest = fused(
        plan, acts, saved_hidden, grad_out, master_reduce, master_expand,
        velocity_reduce, velocity_expand,
    )
    back = lax.dot_general(
        grad_hidden, cur_reduce, (((1,), (1,)), ((), ())), preferred_element_type=f32
    )
    grad_in = (grad_out.astype(f32) + back * inv_c).astype(jnp.bfloat16)
    return (grad_in, *rest)


def solution(mesh):
    rows = P(AXES, None)
    return jax.shard_map(
        functools.partial(shards, Plan(mesh.shape)),
        mesh=mesh,
        in_specs=(rows,) * 7,
        out_specs=(rows,) * 5 + (P(), P()),
        check_vma=False,
    )
```

time: 582 us -> 124 us (0.21)
  waiting for transfers between devices: 488 us -> 0 us
  Pallas kernels: 0 us -> 113 us
  blocking collectives: 37.2 us -> 0 us
  between operations: 17 us -> 0.71 us
  matrix products: 18.4 us -> 4.81 us
  other arithmetic: 7.81 us -> 0 us
  local copies, waits for them, and re-layouts: 12.8 us -> 5.29 us
    reduce_scatter x2 -> x0, waiting for transfers between devices: 268 us -> none  [the longest x1 139 us: shards(): lax.psum_scatter(lax.dot_general(columns, grad_hidden, (((0,), (0,)), (()...]
    all_gather x4 -> x0, waiting for transfers between devices: 219 us -> none  [the longest x1 58.4 us: shards(): lax.all_gather(cur_reduce, ('gx', 'gy', 'gz'), axis=0, tiled=True)]
    pallas_call x0 -> x1, Pallas kernels: none -> 113 us  [fused(): pl.pallas_call(functools.partial(kernel, plan), out_shape=(jax.ShapeDtype...]
    psum x1 -> x0, blocking collectives: 37.2 us -> none  [shards(): lax.psum((reduce_parts[0], reduce_parts[1]), ('gx', 'gy', 'gz'))]
    dot_general x4 -> x1, matrix products: 18.4 us -> 4.81 us  [shards(): lax.dot_general(grad_hidden, cur_reduce, (((1,), (1,)), ((), ())), prefer...]
    unnamed x13 -> x20, local copies, waits for them, and re-layouts: 12.8 us -> 5.29 us
  transfers between devices with their start and end apart: 6 -> 0, of which waited for: 6 -> 0; matrix products, arithmetic and copies ran while one was open for 5% -> 0% of each run, Pallas kernels for 0% -> 0%
where the time goes in v2:
time: 124 us
  Pallas kernels  113 us (91%)
  local copies, waits for them, and re-layouts  5.29 us (4%)
  matrix products  4.81 us (4%)
    pallas_call x1, Pallas kernels, fused(): pl.pallas_call(functools.partial(kernel, plan), out_shape=(jax.ShapeDtype...  113 us
    unnamed x20, local copies, waits for them, and re-layouts  5.29 us
    dot_general x1, matrix products, shards(): lax.dot_general(grad_hidden, cur_reduce, (((1,), (1,)), ((), ())), prefer...  4.81 us

profile of v2, /device:TPU:0, one launch (start us, length us, event | category | flops | bytes accessed | tf_op | source)
XLA Modules:
  0.0 124.2 jit_solution(11112745672373459047)
XLA Ops:
  0.6 0.0 copy-start
  0.6 113.4 %fused_step.1 = (bf16[588,512]{1,0:T(8,128)(2,1)}, bf16[2,2,2,2,2,64,512]{6,5,4,3,2,1,0:T(8,128)(2,1)}, f32[64,512]{1,0:T(8,128)}, f32[64,512]{1,0:T(8,128)}, f3...) custom-call(bf16[588,2048]{1,0:T(8,128)(2,1)} %acts.1, ...), custom_call_target="tpu_custom_call" | custom-call | tf_op jit(solution)/shard_map/fused_step/pallas_call | solution.py:345
  114.1 0.0 copy-done
  114.1 0.0 copy-start.6
  114.1 0.0 copy-start.5
  114.1 0.0 copy-start.4
  114.1 0.0 copy-start.3
  114.1 0.0 copy-start.2
  114.2 4.8 %add_convert_fusion = bf16[588,2048]{1,0:T(8,128)(2,1)} fusion(bf16[588,2048]{1,0:T(8,128)(2,1)S(1)} %copy-done, bf16[588,512]{1,0:T(8,128)(2,1)} %get-tuple-element.15, bf16[2048,512]{1,0:T(8,128)(2,1)} %bitcast.7), kind=kOutput, calls=%fused_computation | convolution fusion | flops 1237942272 | bytes 7516160 | tf_op jit(solution)/shard_map/dot_general | solution.py:381
  119.0 0.0 copy-done.6
  119.0 0.7 copy.20
  119.6 0.0 copy-done.5
  119.6 0.0 copy-start.1
  119.6 0.7 copy.21
  120.3 0.0 copy-done.4
  120.3 0.7 copy.22
  120.9 0.0 copy-done.3
  120.9 0.7 copy.23
  121.6 0.0 copy-done.2
  121.6 1.3 %copy.24 = bf16[2048,512]{1,0:T(8,128)(2,1)} copy(bf16[2048,512]{1,0:T(8,128)(2,1)S(1)} %bitcast.6) | data formatting | bytes 4194304
  122.9 0.0 copy-done.1
  122.9 1.3 %copy.25 = bf16[2048,512]{1,0:T(8,128)(2,1)} copy(bf16[2048,512]{1,0:T(8,128)(2,1)S(1)} %bitcast.5) | data formatting | bytes 4194304
Async XLA Ops:
  0.6 113.5 %copy-start = (bf16[588,2048]{1,0:T(8,128)(2,1)S(1)}, bf16[588,2048]{1,0:T(8,128)(2,1)}, u32[]{:S(2)}) copy-start(bf16[588,2048]{1,0:T(8,128)(2,1)} %grad_out.1) | copy-start | bytes 7225348
  114.1 4.9 %copy-start.6 = (f32[64,512]{1,0:T(8,128)S(1)}, f32[64,512]{1,0:T(8,128)}, u32[]{:S(2)}) copy-start(f32[64,512]{1,0:T(8,128)} %get-tuple-element.31) | copy-start | bytes 393220
  114.1 5.5 %copy-start.5 = (f32[64,512]{1,0:T(8,128)S(1)}, f32[64,512]{1,0:T(8,128)}, u32[]{:S(2)}) copy-start(f32[64,512]{1,0:T(8,128)} %get-tuple-element.32) | copy-start | bytes 393220
  114.1 6.2 %copy-start.4 = (f32[64,512]{1,0:T(8,128)S(1)}, f32[64,512]{1,0:T(8,128)}, u32[]{:S(2)}) copy-start(f32[64,512]{1,0:T(8,128)} %get-tuple-element.33) | copy-start | bytes 393220
  114.1 6.8 %copy-start.3 = (f32[64,512]{1,0:T(8,128)S(1)}, f32[64,512]{1,0:T(8,128)}, u32[]{:S(2)}) copy-start(f32[64,512]{1,0:T(8,128)} %get-tuple-element.34) | copy-start | bytes 393220
  114.1 7.5 %copy-start.2 = (bf16[2,2,2,2,2,64,512]{6,5,4,3,2,1,0:T(8,128)(2,1)S(1)}, bf16[2,2,2,2,2,64,512]{6,5,4,3,2,1,0:T(8,128)(2,1)}, u32[]{:S(2)}) copy-start(bf16[2,2,2,2,2,64,512]{6,5,4,3,2,1,0:T(8,128)(2,1)} %get-tuple-element.21) | copy-start | bytes 6291460
  119.6 3.3 %copy-start.1 = (bf16[2,2,2,2,2,64,512]{6,5,4,3,2,1,0:T(8,128)(2,1)S(1)}, bf16[2,2,2,2,2,64,512]{6,5,4,3,2,1,0:T(8,128)(2,1)}, u32[]{:S(2)}) copy-start(bf16[2,2,2,2,2,64,512]{6,5,4,3,2,1,0:T(8,128)(2,1)} %get-tuple-element.22) | copy-start | bytes 6291460
